TPU v7x, 32 devices: a whole 2x2x4 slice. The times are simulated.
32 devices in a mesh: seq: 8 (over y, x, core), head: 4 (over z).
Axes of the slice: x: 2, y: 2, z: 4, core: 2. Of those that a mesh axis runs over, the one named last changes fastest.
Arguments:
- queries: bfloat16 [8192, 6144], P('seq', 'head'), may hold values from -64 to 64
- text: bfloat16 [512, 6144], P(None, 'seq'), may hold values from -6 to 6
- key_weight: bfloat16 [6144, 6144], P('seq', 'head'), may hold values from -0.078125 to 0.078125
- value_weight: bfloat16 [6144, 6144], P('seq', 'head'), may hold values from -0.078125 to 0.078125
- out_grad: bfloat16 [8192, 6144], P('seq', 'head'), may hold values from -6 to 6
Outputs:
- attn_out: bfloat16 [8192, 6144], P('seq', 'head')
- query_grad: bfloat16 [8192, 6144], P('seq', 'head')
- key_weight_grad: float32 [6144, 6144], P('seq', 'head')
- value_weight_grad: float32 [6144, 6144], P('seq', 'head')
- text_grad: float32 [512, 6144], P('head', 'seq')
All inputs are finite; a program needn't handle non-finite values.
Results may differ from a plain program's by a relative error of at most 0.006.
The roundings to bfloat16 on the way count: a program that leaves them out, or rounds other values in their place, can miss the bound.
Values may be sent and summed in bfloat16 or wider, within the bound.
No kernel may reach another device: no remote copies, remote signals or barrier semaphores. Data moves between devices by JAX's collectives and lax.ppermute only.
A program may use at most 128 MiB of HBM per device.

v0:
```python
import jax
import jax.numpy as jnp
from jax import lax
from jax.sharding import PartitionSpec as P

HS = 128


def local(queries, text, key_weight, value_weight, out_grad):
    row_count = queries.shape[0]
    text_count = text.shape[0]
    head_count = key_weight.shape[1] // HS
    width = key_weight.shape[1]
    score_scale = 1.0 / HS**0.5
    shares = lax.psum_scatter(
        jnp.concatenate(
            [
                jnp.dot(text, key_weight, preferred_element_type=jnp.float32),
                jnp.dot(text, value_weight, preferred_element_type=jnp.float32),
            ],
            axis=1,
        ),
        "seq",
        scatter_dimension=0,
        tiled=True,
    )
    shares_low = shares.astype(jnp.bfloat16)
    both_rows = lax.all_gather(shares_low, "seq", axis=0, tiled=True)
    key_rows = both_rows[:, :width]
    value_rows = both_rows[:, width:]
    query_heads = queries.reshape(row_count, head_count, HS)
    grad_heads = out_grad.reshape(row_count, head_count, HS)
    key_heads = key_rows.reshape(text_count, head_count, HS)
    value_heads = value_rows.reshape(text_count, head_count, HS)
    scores = (
        jnp.einsum("rhd,thd->rht", query_heads, key_heads, preferred_element_type=jnp.float32)
        * score_scale
    )
    probs = jax.nn.softmax(scores, axis=-1)
    probs_low = probs.astype(jnp.bfloat16)
    attn_out = jnp.einsum(
        "rht,thd->rhd", probs_low, value_heads, preferred_element_type=jnp.float32
    )
    attn_out = attn_out.astype(jnp.bfloat16).reshape(row_count, width)
    dprobs = jnp.einsum("rhd,thd->rht", grad_heads, value_heads, preferred_element_type=jnp.float32)
    delta = jnp.sum(probs * dprobs, axis=-1, keepdims=True)
    dscores = (probs * (dprobs - delta) * score_scale).astype(jnp.bfloat16)
    key_term = jnp.einsum("rht,rhd->thd", dscores, query_heads, preferred_element_type=jnp.float32)
    value_term = jnp.einsum(
        "rht,rhd->thd", probs_low, grad_heads, preferred_element_type=jnp.float32
    )
    key_term = key_term.reshape(text_count, width)
    value_term = value_term.reshape(text_count, width)
    key_total, value_total = lax.psum((key_term, value_term), "seq")
    key_grad = key_total.astype(jnp.bfloat16)
    value_grad = value_total.astype(jnp.bfloat16)
    query_grad = jnp.einsum("rht,thd->rhd", dscores, key_heads, preferred_element_type=jnp.float32)
    query_grad = query_grad.astype(jnp.bfloat16).reshape(row_count, width)
    contract_rows = (((0,), (0,)), ((), ()))
    contract_cols = (((1,), (1,)), ((), ()))
    key_weight_grad = lax.dot_general(
        text, key_grad, contract_rows, preferred_element_type=jnp.float32
    )
    value_weight_grad = lax.dot_general(
        text, value_grad, contract_rows, preferred_element_type=jnp.float32
    )
    text_part = lax.dot_general(
        key_grad, key_weight, contract_cols, preferred_element_type=jnp.float32
    ) + lax.dot_general(value_grad, value_weight, contract_cols, preferred_element_type=jnp.float32)
    text_grad = lax.psum_scatter(text_part, "head", scatter_dimension=0, tiled=True)
    return (attn_out, query_grad, key_weight_grad, value_weight_grad, text_grad)


def solution(mesh):
    in_specs = (
        P("seq", "head"),
        P(None, "seq"),
        P("seq", "head"),
        P("seq", "head"),
        P("seq", "head"),
    )
    out_specs = (
        P("seq", "head"),
        P("seq", "head"),
        P("seq", "head"),
        P("seq", "head"),
        P("head", "seq"),
    )
    return jax.shard_map(local, mesh=mesh, in_specs=in_specs, out_specs=out_specs, check_vma=False)
```

profile of v0, /device:TPU:0, one launch (start us, length us, event | category | flops | bytes accessed | tf_op | source)
XLA Modules:
  0.0 419.7 jit_solution(513388792525114465)
XLA Ops:
  7.2 0.0 reduce-scatter.3.cloned.1.call-start
  7.2 1.6 copy-done
  8.8 2.7 fusion.36
  11.5 1.4 fusion.37
  12.9 3.2 pad_maximum_fusion
  16.1 0.0 reduce-scatter.3.cloned.1.call-update
  16.2 0.0 all-gather.2.cloned.1.call-start
  16.2 64.6 %reduce-scatter.3.cloned.1.call-done = f32[64,3072]{1,0:T(8,128)} async-done(((f32[512,3072]{1,0:T(8,128)}), f32[64,3072]{1,0:T(8,128)}) %reduce-scatter.3.cloned.1.call-update) | async-done | bytes 786448 | tf_op jit(solution)/shard_map/reduce_scatter | solution.py:15
  80.8 1.9 convert_element_type.27
  82.7 0.0 all-gather.2.cloned.1.call-update
  82.7 0.2 reduce-scatter.5.cloned.1.call-start
  83.0 4.6 %copy.28 = bf16[1024,1536]{0,1:T(8,128)(2,1)} copy(bf16[1024,1536]{1,0:T(8,128)(2,1)} %param.5) | data formatting | bytes 6291456 | tf_op args[0]
  87.6 4.7 %copy.32 = bf16[1024,1536]{0,1:T(8,128)(2,1)} copy(bf16[1024,1536]{1,0:T(8,128)(2,1)} %param.9) | data formatting | bytes 6291456 | tf_op args[4]
  92.3 23.2 %all-gather.2.cloned.1.call-done = bf16[512,3072]{1,0:T(8,128)(2,1)} async-done(((bf16[64,3072]{1,0:T(8,128)(2,1)}), bf16[512,3072]{1,0:T(8,128)(2,1)}) %all-gather.2.cloned.1.call-update) | async-done | bytes 3145744 | tf_op jit(solution)/shard_map/all_gather | solution.py:28
  115.5 3.7 fusion.34
  119.2 2.6 copy.27
  121.8 2.6 copy.26
  124.4 14.1 %fusion.38 = f32[12,512,1024]{2,1,0:T(8,128)} fusion(bf16[512,12,128]{0,2,1:T(8,128)(2,1)} %bitcast.81, bf16[1024,12,128]{0,2,1:T(8,128)(2,1)} %bitcast.79), kind=kOutput, calls=%fused_computation.42 | convolution fusion | flops 1610612736 | bytes 29884416 | tf_op jit(solution)/shard_map/rhd,thd->rht/dot_general | solution.py:45
  138.5 14.4 %fusion.35 = (f32[1024,12]{0,1:T(8,128)S(1)}, f32[1024,12,512]{0,2,1:T(8,128)}) fusion(bf16[512,12,128]{0,2,1:T(8,128)(2,1)} %bitcast.89, bf16[1024,12,128]{0,2,1:T(8,128)(2,1)} %bitcast.83), kind=kOutput, calls=%fused_computation.39 | convolution fusion | flops 1629487616 | bytes 29933568 | tf_op jit(solution)/shard_map/sub | solution.py:39
  152.9 35.0 %fusion.12 = f32[12,512,128]{1,2,0:T(8,128)} fusion(bf16[1024,12,128]{0,2,1:T(8,128)(2,1)} %bitcast.84, f32[12,512,1024]{2,1,0:T(8,128)} %fusion.38, f32[1024,12,512]{0,2,1:T(8,128)} %get-tuple-element.20, f32[1024,12]{0,1:T(8,128)S(1)} %get-tuple-element.19), kind=kOutput, calls=%fused_computation.15 | convolution fusion | flops 1654665728 | bytes 56672256 | tf_op jit(solution)/shard_map/rht,rhd->thd/dot_general | solution.py:48
  188.0 34.4 %fusion.20 = bf16[12,128,1024]{2,1,0:T(8,128)(2,1)} fusion(bf16[512,12,128]{0,2,1:T(8,128)(2,1)} %bitcast.90, f32[12,512,1024]{2,1,0:T(8,128)} %fusion.38, f32[1024,12,512]{0,2,1:T(8,128)} %get-tuple-element.20, f32[1024,12]{0,1:T(8,128)S(1)} %get-tuple-element.19), kind=kOutput, calls=%fused_computation.25 | convolution fusion | flops 1656238592 | bytes 55099392 | tf_op jit(solution)/shard_map/rht,thd->rhd/dot_general | solution.py:57
  222.4 13.1 %fusion.14 = f32[12,512,128]{1,2,0:T(8,128)} fusion(bf16[1024,12,128]{0,2,1:T(8,128)(2,1)} %bitcast.80, f32[1024,12,512]{0,2,1:T(8,128)} %get-tuple-element.20, f32[1024,12]{0,1:T(8,128)S(1)} %get-tuple-element.19), kind=kOutput, calls=%fused_computation.18 | convolution fusion | flops 1623195648 | bytes 31506432 | tf_op jit(solution)/shard_map/rht,rhd->thd/dot_general | solution.py:49
  235.4 4.6 %copy.39 = bf16[1024,1536]{1,0:T(8,128)(2,1)} copy(bf16[1024,1536]{0,1:T(8,128)(2,1)} %bitcast.87) | data formatting | bytes 6291456
  240.1 128.2 %all-reduce.2 = (bf16[512,1536]{0,1:T(8,128)(2,1)}, bf16[512,1536]{0,1:T(8,128)(2,1)}) all-reduce(f32[512,1536]{0,1:T(8,128)} %bitcast.85, f32[512,1536]{0,1:T(8,128)} %bitcast.86), channel_id=1, replica_groups=mesh['seq'=8,'head'=4] {'seq'}, use_global_device_ids=true, to_apply=%region_4.0 | all-reduce | flops 1572864 | bytes 9437184 | tf_op jit(solution)/shard_map/psum | solution.py:54
  368.3 3.0 fusion.39
  371.3 2.7 convolution_add_fusion
  374.0 12.5 %fusion.21 = bf16[12,128,1024]{2,1,0:T(8,128)(2,1)} fusion(bf16[512,12,128]{0,2,1:T(8,128)(2,1)} %bitcast.82, f32[1024,12,512]{0,2,1:T(8,128)} %get-tuple-element.20, f32[1024,12]{0,1:T(8,128)S(1)} %get-tuple-element.19), kind=kOutput, calls=%fused_computation.26 | convolution fusion | flops 1624768512 | bytes 29933568 | tf_op jit(solution)/shard_map/rht,thd->rhd/dot_general | solution.py:41
  386.5 4.7 %copy.38 = bf16[1024,1536]{1,0:T(8,128)(2,1)} copy(bf16[1024,1536]{0,1:T(8,128)(2,1)} %bitcast.88) | data formatting | bytes 6291456
  391.2 5.0 %convolution_bitcast_fusion = f32[768,1536]{0,1:T(8,128)} fusion(bf16[512,768]{1,0:T(8,128)(2,1)S(1)} %copy-done.2, bf16[512,1536]{0,1:T(8,128)(2,1)} %get-tuple-element.16), kind=kOutput, calls=%fused_computation.22 | convolution fusion | flops 1207959552 | bytes 7077888 | tf_op jit(solution)/shard_map/dot_general | solution.py:64
  396.1 6.1 %copy.41 = f32[768,1536]{1,0:T(8,128)} copy(f32[768,1536]{0,1:T(8,128)} %convolution_bitcast_fusion) | data formatting | bytes 9437184
  402.2 4.9 %convolution_bitcast_fusion.1 = f32[768,1536]{0,1:T(8,128)} fusion(bf16[512,768]{1,0:T(8,128)(2,1)S(1)} %copy-done.2, bf16[512,1536]{0,1:T(8,128)(2,1)} %get-tuple-element.15), kind=kOutput, calls=%fused_computation.23 | convolution fusion | flops 1207959552 | bytes 7077888 | tf_op jit(solution)/shard_map/dot_general | solution.py:61
  407.2 6.1 %copy.40 = f32[768,1536]{1,0:T(8,128)} copy(f32[768,1536]{0,1:T(8,128)} %convolution_bitcast_fusion.1) | data formatting | bytes 9437184
  (13 shorter events, 0.0 us)
Async XLA Ops:
  7.2 1.7 copy-start
  7.2 4.3 %copy-start.1 = (bf16[512,768]{1,0:T(8,128)(2,1)S(1)}, bf16[512,768]{1,0:T(8,128)(2,1)}, u32[]{:S(2)}) copy-start(bf16[512,768]{1,0:T(8,128)(2,1)} %param.6) | copy-start | bytes 2359300
  7.2 73.6 %reduce-scatter.3.cloned.1.call-start = ((), (), s32[]{:S(2)}) async-start(), calls=%async_computation.2 | async-start | bytes 7077888 | tf_op jit(solution)/shard_map/reduce_scatter | solution.py:15
  8.8 2.7 copy-start.4
  16.2 99.3 %all-gather.2.cloned.1.call-start = ((), (), s32[]{:S(2)}) async-start(), calls=%async_computation.3 | async-start | bytes 3538944 | tf_op jit(solution)/shard_map/all_gather | solution.py:28
  82.7 330.5 %reduce-scatter.5.cloned.1.call-start = ((), (), s32[]{:S(2)}) async-start(), calls=%async_computation.4 | async-start | bytes 1966080 | tf_op jit(solution)/shard_map/reduce_scatter | solution.py:70
  368.3 3.0 copy-start.3
  368.3 3.0 copy-start.5
  386.4 4.7 %copy-start.2 = (bf16[512,768]{1,0:T(8,128)(2,1)S(1)}, bf16[512,768]{1,0:T(8,128)(2,1)}, u32[]{:S(2)}) copy-start(bf16[512,768]{1,0:T(8,128)(2,1)} %param.6) | copy-start | bytes 2359300
Sparse Core Ops, SparseCore 0:
  16.3 64.4 reduce-scatter.2
  83.2 32.1 all-gather.1
  374.1 35.3 reduce-scatter.4
where the time goes:
time: 421 us; the launch traced here: 420 us
  matrix products  143 us (34%)
  blocking collectives  128 us (30%)
  waiting for transfers between devices  87.8 us (21%)
  local copies, waits for them, and re-layouts  41.4 us (10%)
  between operations  13.8 us (3%)
  other arithmetic  5.14 us (1%)
    psum x1, blocking collectives, local(): key_total, value_total = lax.psum((key_term, value_term), 'seq')  128 us
    reduce_scatter x1, waiting for transfers between devices, local(): lax.psum_scatter(jnp.concatenate([jnp.dot(text, key_weight, preferred_ele...  64.6 us
    dot_general x1, matrix products, local(): jnp.einsum('rht,rhd->thd', dscores, query_heads, preferred_element_type=j...  35 us
    dot_general x1, matrix products, local(): jnp.einsum('rht,thd->rhd', dscores, key_heads, preferred_element_type=jnp...  34.4 us
    unnamed x18, local copies, waits for them, and re-layouts  32.4 us
    all_gather x1, waiting for transfers between devices, local(): both_rows = lax.all_gather(shares_low, 'seq', axis=0, tiled=True)  23.2 us
    sub x1, matrix products, local(): probs = jax.nn.softmax(scores, axis=-1)  14.4 us
    dot_general x1, matrix products, local(): jnp.einsum('rhd,thd->rht', grad_heads, value_heads, preferred_element_typ...  14.1 us
  transfers between devices with their start and end apart: 3, of which 2 were waited for; matrix products, arithmetic and copies ran while one was open for 12% of the time, Pallas kernels for 0%

commit v1 on v0

v1 whole, which is shorter than its diff:
```python
import functools
import math

import jax
import jax.numpy as jnp
from jax import lax
from jax.experimental import pallas as pl
from jax.experimental.pallas import tpu as pltpu
from jax.sharding import PartitionSpec as P

HS = 128
SCALE = 1.0 / HS**0.5
LOG2E = math.log2(math.e)
F32 = jnp.float32
BF16 = jnp.bfloat16
NT = (((1,), (1,)), ((), ()))
NN = (((1,), (0,)), ((), ()))


def dot(a, b, dims=NN):
    return lax.dot_general(a, b, dims, preferred_element_type=F32)


def swap(x, axis, size, bit):
    return lax.ppermute(x, axis, [(j, j ^ (1 << bit)) for j in range(size)])


def mask_of(position, order):
    mask = position * 0
    for k, bit in enumerate(order):
        mask = mask | (((position >> (len(order) - 1 - k)) & 1) << bit)
    return mask


def position_of(mask, order):
    position = mask * 0
    for k, bit in enumerate(order):
        position = position | (((mask >> bit) & 1) << (len(order) - 1 - k))
    return position


def project(text, key_weight, value_weight, blocks, first_col, heads, step_heads):
    tokens, depth = text.shape
    count = blocks.shape[0]
    size = tokens // count
    half = tokens // 2
    cols = step_heads * HS
    steps = heads // step_heads
    offset = first_col // cols

    def body(blocks_ref, text_ref, kw_ref, vw_ref, keep_ref, send_ref, order_ref):
        @pl.when(pl.program_id(0) == 0)
        def _():
            for p in range(count):
                start = pl.multiple_of(blocks_ref[p] * size, size)
                order_ref[p * size : (p + 1) * size, :] = text_ref[pl.ds(start, size), :]

        rows = order_ref[...]
        for index, w_ref in enumerate((kw_ref, vw_ref)):
            part = dot(rows, w_ref[...])
            keep_ref[index] = part[:half]
            send_ref[index] = part[half:]

    shape = jax.ShapeDtypeStruct((2, half, heads * HS), F32)
    block = pl.BlockSpec((2, half, cols), lambda j, b: (0, 0, j))
    weight = pl.BlockSpec((depth, cols), lambda j, b: (0, offset + j))
    return pl.pallas_call(
        body,
        out_shape=(shape, shape),
        grid_spec=pltpu.PrefetchScalarGridSpec(
            num_scalar_prefetch=1,
            grid=(steps,),
            in_specs=[pl.BlockSpec((tokens, depth), lambda j, b: (0, 0)), weight, weight],
            out_specs=[block, block],
            scratch_shapes=[pltpu.VMEM((tokens, depth), BF16)],
        ),
        compiler_params=pltpu.CompilerParams(dimension_semantics=("arbitrary",)),
        cost_estimate=pl.CostEstimate(
            flops=4 * tokens * depth * heads * HS, transcendentals=0, bytes_accessed=0
        ),
        name="project",
    )(blocks, text, key_weight, value_weight)


def attend(queries, out_grad, low, high, first_head, previous):
    rows, width = queries.shape
    half, cols = low.shape[1:]
    heads = cols // HS
    chunk = min(rows, 256)

    def body(q_ref, g_ref, low_ref, high_ref, *refs):
        o_ref, dq_ref, keep_ref, send_ref = refs[-4:]
        k = jnp.concatenate([low_ref[0], high_ref[0]], axis=0)
        v = jnp.concatenate([low_ref[1], high_ref[1]], axis=0)
        k_t = k.T
        v_t = v.T
        dk = None
        dv = None
        for c in range(rows // chunk):
            span = slice(c * chunk, (c + 1) * chunk)
            q = q_ref[span, :]
            g = g_ref[span, :]
            s = dot(k, q, NT)
            top = jnp.max(s, axis=0, keepdims=True)
            e = jnp.exp2((s - top) * (SCALE * LOG2E))
            p = e * (1.0 / jnp.sum(e, axis=0, keepdims=True))
            p_low = p.astype(BF16)
            dp = dot(v, g, NT)
            delta = jnp.sum(p * dp, axis=0, keepdims=True)
            ds = (p * (dp - delta) * SCALE).astype(BF16)
            dv_part = dot(p_low, g)
            dk_part = dot(ds, q)
            dv = dv_part if dv is None else dv + dv_part
            dk = dk_part if dk is None else dk + dk_part
            o_ref[span, :] = dot(v_t, p_low).astype(BF16).T
            dq_ref[span, :] = dot(k_t, ds).astype(BF16).T
        keep_ref[0] = dk[:half]
        keep_ref[1] = dv[:half]
        send_ref[0] = dk[half:].astype(BF16)
        send_ref[1] = dv[half:].astype(BF16)

    wide = pl.BlockSpec((rows, HS), lambda h: (0, first_head + h))
    narrow = pl.BlockSpec((2, half, HS), lambda h: (0, 0, h))
    big = jax.ShapeDtypeStruct((rows, width), BF16)
    args = [queries, out_grad, low, high]
    in_specs = [wide, wide, narrow, narrow]
    aliases = {}
    if previous is not None:
        aliases = {len(args): 0, len(args) + 1: 1}
        args += list(previous)
        in_specs += [pl.BlockSpec(memory_space=pl.ANY)] * 2
    return pl.pallas_call(
        body,
        out_shape=(
            big,
            big,
            jax.ShapeDtypeStruct((2, half, cols), F32),
            jax.ShapeDtypeStruct((2, half, cols), BF16),
        ),
        grid=(heads,),
        in_specs=in_specs,
        out_specs=[wide, wide, narrow, narrow],
        input_output_aliases=aliases,
        compiler_params=pltpu.CompilerParams(dimension_semantics=("arbitrary",)),
        cost_estimate=pl.CostEstimate(
            flops=24 * rows * half * cols, transcendentals=0, bytes_accessed=0
        ),
        name="attend",
    )(*args)


def text_grads(key_weight, value_weight, low, high, places, size, first_col, step_heads, previous):
    depth = key_weight.shape[0]
    half, total = low.shape[1:]
    tokens = 2 * half
    cols = step_heads * HS
    offset = first_col // cols

    def body(places_ref, kw_ref, vw_ref, low_ref, high_ref, *refs):
        out_ref = refs[-1]

        @pl.when(pl.program_id(0) == 0)
        def _():
            out_ref[...] = jnp.zeros_like(out_ref) if previous is None else refs[0][...]

        for side, ref in enumerate((low_ref, high_ref)):
            part = dot(ref[0], kw_ref[...], NT) + dot(ref[1], vw_ref[...], NT)
            for j in range(half // size):
                start = pl.multiple_of(places_ref[side * (half // size) + j] * size, size)
                out_ref[pl.ds(start, size), :] += part[j * size : (j + 1) * size]

    weight = pl.BlockSpec((depth, cols), lambda j, a: (0, offset + j))
    narrow = pl.BlockSpec((2, half, cols), lambda j, a: (0, 0, j))
    fixed = pl.BlockSpec((tokens, depth), lambda j, a: (0, 0))
    return pl.pallas_call(
        body,
        out_shape=jax.ShapeDtypeStruct((tokens, depth), F32),
        grid_spec=pltpu.PrefetchScalarGridSpec(
            num_scalar_prefetch=1,
            grid=(total // cols,),
            in_specs=[weight, weight, narrow, narrow] + ([] if previous is None else [fixed]),
            out_specs=fixed,
        ),
        compiler_params=pltpu.CompilerParams(dimension_semantics=("arbitrary",)),
        cost_estimate=pl.CostEstimate(
            flops=4 * tokens * depth * total, transcendentals=0, bytes_accessed=0
        ),
        name="text_grads",
    )(places, key_weight, value_weight, low, high, *(() if previous is None else (previous,)))


def weight_grads(text, low, high, blocks, width, first_col, step_heads, previous):
    tokens, depth = text.shape
    half, total = low.shape[1:]
    cols = step_heads * HS
    offset = first_col // cols
    count = blocks.shape[0]
    size = tokens // count

    def body(blocks_ref, text_ref, low_ref, high_ref, *refs):
        kwg_ref, vwg_ref, order_ref, low_t, high_t = refs[-5:]

        @pl.when(pl.program_id(0) == 0)
        def _():
            for p in range(count):
                start = pl.multiple_of(blocks_ref[p] * size, size)
                order_ref[p * size : (p + 1) * size, :] = text_ref[pl.ds(start, size), :]
            low_t[...] = order_ref[:half, :].T
            high_t[...] = order_ref[half:, :].T

        for index, out_ref in enumerate((kwg_ref, vwg_ref)):
            out_ref[...] = dot(low_t[...], low_ref[index]) + dot(high_t[...], high_ref[index])

    big = jax.ShapeDtypeStruct((depth, width), F32)
    weight = pl.BlockSpec((depth, cols), lambda j, a: (0, offset + j))
    narrow = pl.BlockSpec((2, half, cols), lambda j, a: (0, 0, j))
    args = [blocks, text, low, high]
    in_specs = [pl.BlockSpec((tokens, depth), lambda j, a: (0, 0)), narrow, narrow]
    aliases = {}
    if previous is not None:
        aliases = {len(args): 0, len(args) + 1: 1}
        args += list(previous)
        in_specs += [pl.BlockSpec(memory_space=pl.ANY)] * 2
    return pl.pallas_call(
        body,
        out_shape=(big, big),
        grid_spec=pltpu.PrefetchScalarGridSpec(
            num_scalar_prefetch=1,
            grid=(total // cols,),
            in_specs=in_specs,
            out_specs=[weight, weight],
            scratch_shapes=[
                pltpu.VMEM((tokens, depth), BF16),
                pltpu.VMEM((depth, half), BF16),
                pltpu.VMEM((depth, half), BF16),
            ],
        ),
        input_output_aliases=aliases,
        compiler_params=pltpu.CompilerParams(dimension_semantics=("arbitrary",)),
        cost_estimate=pl.CostEstimate(
            flops=4 * tokens * depth * total, transcendentals=0, bytes_accessed=0
        ),
        name="weight_grads",
    )(*args)


def gather_low(share, size, order):
    for bit in order[:0:-1]:
        share = jnp.concatenate([share, swap(share, "seq", size, bit)], axis=1)
    return share, swap(share, "seq", size, order[0])


def sum_rows(keep, send, size, order):
    total = keep + swap(send, "seq", size, order[0])
    for bit in order[1:]:
        half = total.shape[1] // 2
        keys = swap(total[0, half:], "seq", size, bit)
        values = swap(total[1, half:].astype(BF16), "seq", size, bit).astype(F32)
        total = total[:, :half] + jnp.stack([keys, values])
    return total.astype(BF16)


def sum_grads(keep, send, size, order):
    total = keep + swap(send, "seq", size, order[0]).astype(F32)
    for bit in order[1:]:
        half = total.shape[1] // 2
        total = total[:, :half] + swap(total[:, half:].astype(BF16), "seq", size, bit).astype(F32)
    return total.astype(BF16)


def local(seq_size, head_size, queries, text, key_weight, value_weight, out_grad):
    tokens = text.shape[0]
    heads = key_weight.shape[1] // HS
    seq_bits = list(range(seq_size.bit_length() - 1))
    head_bits = list(range(head_size.bit_length() - 1))
    orders = (seq_bits, seq_bits[:1] + seq_bits[:0:-1])
    first = ((heads + 1) // 2, heads // 2)
    starts = (0, first[0])
    step_heads = math.gcd(*first)
    seq_at = lax.axis_index("seq")
    head_at = lax.axis_index("head")
    places = jnp.arange(seq_size, dtype=jnp.int32)

    blocks = [seq_at ^ mask_of(places, order) for order in orders]
    parts = [
        project(text, key_weight, value_weight, block, start * HS, count, step_heads)
        for block, count, start in zip(blocks, first, starts)
    ]
    shares = [sum_rows(*part, seq_size, order) for part, order in zip(parts, orders)]
    halves = [gather_low(share, seq_size, order) for share, order in zip(shares, orders)]

    wide = None
    grads = []
    for half, start in zip(halves, starts):
        *wide, keep, send = attend(queries, out_grad, *half, start, wide)
        grads.append((keep, send))
    shares = [sum_grads(*grad, seq_size, order) for grad, order in zip(grads, orders)]
    halves = [gather_low(share, seq_size, order) for share, order in zip(shares, orders)]

    size = tokens // max(seq_size, head_size)
    slots = jnp.arange(tokens // size, dtype=jnp.int32)
    per_head = tokens // head_size // size
    per_seq = tokens // seq_size // size
    total = None
    for half, block, start in zip(halves, blocks, starts):
        natural = block[slots // per_seq] * per_seq + slots % per_seq
        spot = position_of(head_at ^ (natural // per_head), head_bits)
        target = spot * per_head + natural % per_head
        total = text_grads(
            key_weight, value_weight, *half, target, size, start * HS, step_heads, total
        )
    weights = None
    for half, block, start in zip(halves, blocks, starts):
        weights = weight_grads(text, *half, block, heads * HS, start * HS, step_heads, weights)
    for bit in head_bits:
        half = total.shape[0] // 2
        total = total[:half] + swap(total[half:].astype(BF16), "head", head_size, bit).astype(F32)
    return (*wide, *weights, total)


def solution(mesh):
    in_specs = (
        P("seq", "head"),
        P(None, "seq"),
        P("seq", "head"),
        P("seq", "head"),
        P("seq", "head"),
    )
    out_specs = (
        P("seq", "head"),
        P("seq", "head"),
        P("seq", "head"),
        P("seq", "head"),
        P("head", "seq"),
    )
    body = functools.partial(local, mesh.shape["seq"], mesh.shape["head"])
    return jax.shard_map(body, mesh=mesh, in_specs=in_specs, out_specs=out_specs, check_vma=False)
```

time: 421 us -> 190 us (0.45)
  matrix products: 143 us -> 0 us
  blocking collectives: 128 us -> 0 us
  Pallas kernels: 0 us -> 71.7 us
  local copies, waits for them, and re-layouts: 41.4 us -> 6.45 us
  starting transfers between devices: 0.3 us -> 32.5 us
  waiting for transfers between devices: 87.8 us -> 72.4 us
  between operations: 13.8 us -> 1.03 us
    dot_general x11 -> x0, matrix products: 129 us -> none  [the longest x1 35 us: local(): jnp.einsum('rht,rhd->thd', dscores, query_heads, preferred_element_type=j...]
    psum x1 -> x0, blocking collectives: 128 us -> none  [local(): key_total, value_total = lax.psum((key_term, value_term), 'seq')]
    ppermute x0 -> x30, waiting for transfers between devices: none -> 72.4 us  [swap(): return lax.ppermute(x, axis, [(j, j ^ 1 << bit) for j in range(size)])]
    pallas_call x0 -> x8, Pallas kernels: none -> 71.7 us  [the longest x2 38.5 us: attend(): pl.pallas_call(body, out_shape=(big, big, jax.ShapeDtypeStruct((2, half,...]
    reduce_scatter x2 -> x0, waiting for transfers between devices: 64.6 us -> none  [the longest x1 64.6 us: local(): lax.psum_scatter(jnp.concatenate([jnp.dot(text, key_weight, preferred_ele...]
    ppermute x0 -> x30, starting transfers between devices: none -> 32.5 us  [swap(): return lax.ppermute(x, axis, [(j, j ^ 1 << bit) for j in range(size)])]
    unnamed x18 -> x28, local copies, waits for them, and re-layouts: 32.4 us -> 3.68 us
    all_gather x1 -> x0, waiting for transfers between devices: 23.2 us -> none  [local(): both_rows = lax.all_gather(shares_low, 'seq', axis=0, tiled=True)]
  transfers between devices with their start and end apart: 3 -> 30, of which waited for: 2 -> 19; matrix products, arithmetic and copies ran while one was open for 12% -> 2% of each run, Pallas kernels for 0% -> 32%
where the time goes in v1:
time: 190 us
  waiting for transfers between devices  72.4 us (38%)
  Pallas kernels  71.7 us (38%)
  starting transfers between devices  32.5 us (17%)
  local copies, waits for them, and re-layouts  6.45 us (3%)
  other arithmetic  5.71 us (3%)
    ppermute x30, waiting for transfers between devices, swap(): return lax.ppermute(x, axis, [(j, j ^ 1 << bit) for j in range(size)])  72.4 us
    pallas_call x2, Pallas kernels, attend(): pl.pallas_call(body, out_shape=(big, big, jax.ShapeDtypeStruct((2, half,...  38.5 us
    ppermute x30, starting transfers between devices, swap(): return lax.ppermute(x, axis, [(j, j ^ 1 << bit) for j in range(size)])  32.5 us
    pallas_call x2, Pallas kernels, text_grads(): pl.pallas_call(body, out_shape=jax.ShapeDtypeStruct((tokens, depth), F32)...  11.2 us
    pallas_call x2, Pallas kernels, project(): pl.pallas_call(body, out_shape=(shape, shape), grid_spec=pltpu.PrefetchSc...  11.1 us
    pallas_call x2, Pallas kernels, weight_grads(): pl.pallas_call(body, out_shape=(big, big), grid_spec=pltpu.PrefetchScalar...  10.9 us
  transfers between devices with their start and end apart: 30, of which 19 were waited for; matrix products, arithmetic and copies ran while one was open for 2% of the time, Pallas kernels for 32%

profile of v1, /device:TPU:0, one launch (start us, length us, event | category | flops | bytes accessed | tf_op | source)
XLA Modules:
  0.0 189.8 jit_solution(14022250686004693189)
XLA Ops:
  1.2 5.5 %project.2 = (f32[2,256,768]{2,1,0:T(8,128)}, f32[2,256,768]{2,1,0:T(8,128)}) custom-call(s32[8]{0:T(128)} %or_xor_fusion.1.blocks_ref, bf16[512,768]{1,0:T(8,128)(2,1)} %text_ref.7, bf16[768,1536]{1,0:T(8,128)(2,1)} %kw_ref.7, bf16[768,1536]{1,0:T(8,128)(2,1)} %vw_ref.7), custom_call_target="tpu_custom_call" | custom-call | flops 1207959552 | tf_op jit(solution)/shard_map/project/pallas_call | solution.py:67
  7.7 5.6 %project.3 = (f32[2,256,768]{2,1,0:T(8,128)}, f32[2,256,768]{2,1,0:T(8,128)}) custom-call(s32[8]{0:T(128)} %or_xor_fusion.blocks_ref, bf16[512,768]{1,0:T(8,128)(2,1)} %text_ref.7, bf16[768,1536]{1,0:T(8,128)(2,1)} %kw_ref.7, bf16[768,1536]{1,0:T(8,128)(2,1)} %vw_ref.7), custom_call_target="tpu_custom_call" | custom-call | flops 1207959552 | tf_op jit(solution)/shard_map/project/pallas_call | solution.py:67
  13.6 3.1 %collective-permute-start.2 = (bf16[128,768]{1,0:T(8,128)(2,1)S(1)}, bf16[128,768]{1,0:T(8,128)(2,1)S(1)}, u32[]{:S(2)}, u32[]{:S(2)}) collective-permute-start(bf16[128,768]{1,0:T(8,128)(2,1)S(1)} %fusion.4), channel_id=1, source_target_pairs={{0,16},{4,20},{8,24},{12,28},{16,0},{20,4},{24,8},{28,12},{1,17},{... | collective-permute-start | bytes 589832 | tf_op jit(solution)/shard_map/ppermute | solution.py:25
  17.2 2.7 %collective-permute-start.10 = (bf16[128,768]{1,0:T(8,128)(2,1)S(1)}, bf16[128,768]{1,0:T(8,128)(2,1)S(1)}, u32[]{:S(2)}, u32[]{:S(2)}) collective-permute-start(bf16[128,768]{1,0:T(8,128)(2,1)S(1)} %fusion.5), channel_id=1, source_target_pairs={{0,8},{4,12},{8,0},{12,4},{16,24},{20,28},{24,16},{28,20},{1,9},{5... | collective-permute-start | bytes 589832 | tf_op jit(solution)/shard_map/ppermute | solution.py:25
  20.0 2.4 %collective-permute-done.2 = bf16[128,768]{1,0:T(8,128)(2,1)S(1)} collective-permute-done((bf16[128,768]{1,0:T(8,128)(2,1)S(1)}, bf16[128,768]{1,0:T(8,128)(2,1)S(1)}, u32[]{:S(2)}, u32[]{:S(2)}) %collective-permute-start.2) | collective-permute-done | bytes 196640 | tf_op jit(solution)/shard_map/ppermute | solution.py:25
  22.4 3.2 %collective-permute-done.10 = bf16[128,768]{1,0:T(8,128)(2,1)S(1)} collective-permute-done((bf16[128,768]{1,0:T(8,128)(2,1)S(1)}, bf16[128,768]{1,0:T(8,128)(2,1)S(1)}, u32[]{:S(2)}, u32[]{:S(2)}) %collective-permute-start.10) | collective-permute-done | bytes 196640 | tf_op jit(solution)/shard_map/ppermute | solution.py:25
  25.6 8.1 %collective-permute-done.9 = f32[128,768]{1,0:T(8,128)S(1)} collective-permute-done((f32[128,768]{1,0:T(8,128)S(1)}, f32[128,768]{1,0:T(8,128)S(1)}, u32[]{:S(2)}, u32[]{:S(2)}) %collective-permute-start.9) | collective-permute-done | bytes 393248 | tf_op jit(solution)/shard_map/ppermute | solution.py:25
  34.0 1.8 collective-permute-start.12
  35.9 1.6 collective-permute-start.4
  38.7 4.9 %collective-permute-done.11 = f32[64,768]{1,0:T(8,128)S(1)} collective-permute-done((f32[64,768]{1,0:T(8,128)S(1)}, f32[64,768]{1,0:T(8,128)S(1)}, u32[]{:S(2)}, u32[]{:S(2)}) %collective-permute-start.11) | collective-permute-done | bytes 196640 | tf_op jit(solution)/shard_map/ppermute | solution.py:25
  44.8 4.6 %collective-permute-done.13 = bf16[2,64,768]{2,1,0:T(8,128)(2,1)S(1)} collective-permute-done((bf16[2,64,768]{2,1,0:T(8,128)(2,1)S(1)}, bf16[2,64,768]{2,1,0:T(8,128)(2,1)S(1)}, u32[]{:S(2)}, u32[]{:S(2)}) %collective-permute-start.13) | collective-permute-done | bytes 196640 | tf_op jit(solution)/shard_map/ppermute | solution.py:25
  49.4 1.6 collective-permute-start.14
  51.7 10.0 %collective-permute-done.5 = bf16[2,64,768]{2,1,0:T(8,128)(2,1)S(1)} collective-permute-done((bf16[2,64,768]{2,1,0:T(8,128)(2,1)S(1)}, bf16[2,64,768]{2,1,0:T(8,128)(2,1)S(1)}, u32[]{:S(2)}, u32[]{:S(2)}) %collective-permute-start.5) | collective-permute-done | bytes 196640 | tf_op jit(solution)/shard_map/ppermute | solution.py:25
  61.7 1.8 collective-permute-start.6
  63.7 5.9 %collective-permute-done.6 = bf16[2,128,768]{2,1,0:T(8,128)(2,1)S(1)} collective-permute-done((bf16[2,128,768]{2,1,0:T(8,128)(2,1)S(1)}, bf16[2,128,768]{2,1,0:T(8,128)(2,1)S(1)}, u32[]{:S(2)}, u32[]{:S(2)}) %collective-permute-start.6) | collective-permute-done | bytes 393248 | tf_op jit(solution)/shard_map/ppermute | solution.py:25
  70.8 19.1 %attend.2 = (bf16[1024,1536]{1,0:T(8,128)(2,1)}, bf16[1024,1536]{1,0:T(8,128)(2,1)}, f32[2,256,768]{2,1,0:T(8,128)}, bf16[2,256,768]{2,1,0:T(8,128)(2,1)}) custom-call(bf16[1024,1536]{1,0:T(8,128)(2,1)} %q_ref.3, bf16[1024,1536]{1,0:T(8,128)(2,1)} %g_ref.3, bf16[2,256,768]{2,1,0:T(8,128)(2,1)} %copy-done.10, bf16[2,256,768]{2,1,0:T(8,128)(2,1)} %copy-done.13), custom_call_target="tpu_custom_call" | custom-call | flops 4831838208 | tf_op jit(solution)/shard_map/attend/pallas_call | solution.py:132
  91.2 19.3 %attend.3 = (bf16[1024,1536]{1,0:T(8,128)(2,1)}, bf16[1024,1536]{1,0:T(8,128)(2,1)}, f32[2,256,768]{2,1,0:T(8,128)}, bf16[2,256,768]{2,1,0:T(8,128)(2,1)}) custom-call(bf16[1024,1536]{1,0:T(8,128)(2,1)} %q_ref.3, bf16[1024,1536]{1,0:T(8,128)(2,1)} %g_ref.3, bf16[2,256,768]{2,1,0:T(8,128)(2,1)} %copy-done.9, ...), custom_call_target="tpu_custom_call", output_to_operand_aliasing={{0}: (4, {}), {1}: (5, {})} | custom-call | flops 4831838208 | tf_op jit(solution)/shard_map/attend/pallas_call | solution.py:132
  113.3 1.8 collective-permute-start.17
  115.1 7.3 %collective-permute-done.23 = bf16[2,128,768]{2,1,0:T(8,128)(2,1)S(1)} collective-permute-done((bf16[2,128,768]{2,1,0:T(8,128)(2,1)S(1)}, bf16[2,128,768]{2,1,0:T(8,128)(2,1)S(1)}, u32[]{:S(2)}, u32[]{:S(2)}) %collective-permute-start.23) | collective-permute-done | bytes 393248 | tf_op jit(solution)/shard_map/ppermute | solution.py:25
  122.5 1.8 collective-permute-start.24
  125.9 3.0 %collective-permute-done.24 = bf16[2,64,768]{2,1,0:T(8,128)(2,1)S(1)} collective-permute-done((bf16[2,64,768]{2,1,0:T(8,128)(2,1)S(1)}, bf16[2,64,768]{2,1,0:T(8,128)(2,1)S(1)}, u32[]{:S(2)}, u32[]{:S(2)}) %collective-permute-start.24) | collective-permute-done | bytes 196640 | tf_op jit(solution)/shard_map/ppermute | solution.py:25
  128.9 1.8 collective-permute-start.25
  132.1 2.5 %collective-permute-done.25 = bf16[2,64,768]{2,1,0:T(8,128)(2,1)S(1)} collective-permute-done((bf16[2,64,768]{2,1,0:T(8,128)(2,1)S(1)}, bf16[2,64,768]{2,1,0:T(8,128)(2,1)S(1)}, u32[]{:S(2)}, u32[]{:S(2)}) %collective-permute-start.25) | collective-permute-done | bytes 196640 | tf_op jit(solution)/shard_map/ppermute | solution.py:25
  136.0 2.4 %collective-permute-done.19 = bf16[2,64,768]{2,1,0:T(8,128)(2,1)S(1)} collective-permute-done((bf16[2,64,768]{2,1,0:T(8,128)(2,1)S(1)}, bf16[2,64,768]{2,1,0:T(8,128)(2,1)S(1)}, u32[]{:S(2)}, u32[]{:S(2)}) %collective-permute-start.19) | collective-permute-done | bytes 196640 | tf_op jit(solution)/shard_map/ppermute | solution.py:25
  138.4 1.8 collective-permute-start.20
  140.2 4.9 %collective-permute-done.26 = bf16[2,128,768]{2,1,0:T(8,128)(2,1)S(1)} collective-permute-done((bf16[2,128,768]{2,1,0:T(8,128)(2,1)S(1)}, bf16[2,128,768]{2,1,0:T(8,128)(2,1)S(1)}, u32[]{:S(2)}, u32[]{:S(2)}) %collective-permute-start.26) | collective-permute-done | bytes 393248 | tf_op jit(solution)/shard_map/ppermute | solution.py:25
  149.7 5.4 %text_grads.2.refs_0_ = f32[512,768]{1,0:T(8,128)} custom-call(s32[8]{0:T(128)} %fusion.9.places_ref, bf16[768,1536]{1,0:T(8,128)(2,1)} %kw_ref.7, bf16[768,1536]{1,0:T(8,128)(2,1)} %vw_ref.7, bf16[2,256,768]{2,1,0:T(8,128)(2,1)} %copy-done.4, bf16[2,256,768]{2,1,0:T(8,128)(2,1)} %copy-done.11), custom_call_target="tpu_custom_call" | custom-call | flops 1207959552 | tf_op jit(solution)/shard_map/text_grads/pallas_call | solution.py:175
  155.9 5.9 %text_grads.3 = f32[512,768]{1,0:T(8,128)} custom-call(s32[8]{0:T(128)} %fusion.8.places_ref, bf16[768,1536]{1,0:T(8,128)(2,1)} %kw_ref.7, bf16[768,1536]{1,0:T(8,128)(2,1)} %vw_ref.7, bf16[2,256,768]{2,1,0:T(8,128)(2,1)} %copy-done.2, bf16[2,256,768]{2,1,0:T(8,128)(2,1)} %copy-done.3, f32[512,768]{1,0:T(8,128)} %text_grads.2.refs_0_), custom_call_target="tpu_custom_call" | custom-call | flops 1207959552 | tf_op jit(solution)/shard_map/text_grads/pallas_call | solution.py:175
  164.3 10.2 %collective-permute-done.28 = bf16[256,768]{1,0:T(8,128)(2,1)S(1)} collective-permute-done((bf16[256,768]{1,0:T(8,128)(2,1)S(1)}, bf16[256,768]{1,0:T(8,128)(2,1)S(1)}, u32[]{:S(2)}, u32[]{:S(2)}) %collective-permute-start.28) | collective-permute-done | bytes 393248 | tf_op jit(solution)/shard_map/ppermute | solution.py:25
  175.8 2.3 %collective-permute-start.29 = (bf16[128,768]{1,0:T(8,128)(2,1)S(1)}, bf16[128,768]{1,0:T(8,128)(2,1)S(1)}, u32[]{:S(2)}, u32[]{:S(2)}) collective-permute-start(bf16[128,768]{1,0:T(8,128)(2,1)S(1)} %slice.177), channel_id=1, source_target_pairs={{0,2},{1,3},{2,0},{3,1},{4,6},{5,7},{6,4},{7,5},{8,10},{9,11},{10,... | collective-permute-start | bytes 589832 | tf_op jit(solution)/shard_map/ppermute | solution.py:25
  178.1 5.5 %weight_grads.2 = (f32[768,1536]{1,0:T(8,128)}, f32[768,1536]{1,0:T(8,128)}) custom-call(s32[8]{0:T(128)} %or_xor_fusion.blocks_ref, bf16[512,768]{1,0:T(8,128)(2,1)} %text_ref.7, bf16[2,256,768]{2,1,0:T(8,128)(2,1)} %copy-done.4, bf16[2,256,768]{2,1,0:T(8,128)(2,1)} %copy-done.11), custom_call_target="tpu_custom_call" | custom-call | flops 1207959552 | tf_op jit(solution)/shard_map/weight_grads/pallas_call | solution.py:224
  183.6 5.5 %weight_grads.3 = (f32[768,1536]{1,0:T(8,128)}, f32[768,1536]{1,0:T(8,128)}) custom-call(s32[8]{0:T(128)} %or_xor_fusion.1.blocks_ref, bf16[512,768]{1,0:T(8,128)(2,1)} %text_ref.7, bf16[2,256,768]{2,1,0:T(8,128)(2,1)} %copy-done.2, bf16[2,256,768]{2,1,0:T(8,128)(2,1)} %copy-done.3, ...), custom_call_target="tpu_custom_call", output_to_operand_aliasing={{0}: (4, {}), {1}: (5, {})} | custom-call | flops 1207959552 | tf_op jit(solution)/shard_map/weight_grads/pallas_call | solution.py:224
  (112 shorter events, 25.6 us)
Async XLA Ops:
  6.7 6.7 %collective-permute-start = (f32[2,256,768]{2,1,0:T(8,128)}, f32[2,256,768]{2,1,0:T(8,128)S(1)}, u32[]{:S(2)}, u32[]{:S(2)}) collective-permute-start(f32[2,256,768]{2,1,0:T(8,128)} %get-tuple-element.22), channel_id=1, source_target_pairs={{0,4},{4,0},{8,12},{12,8},{16,20},{20,16},{24,28},{28,24},{1,5},{5... | collective-permute-start | bytes 4718600 | tf_op jit(solution)/shard_map/ppermute | solution.py:25
  13.3 3.6 %collective-permute-start.8 = (f32[2,256,768]{2,1,0:T(8,128)}, f32[2,256,768]{2,1,0:T(8,128)S(1)}, u32[]{:S(2)}, u32[]{:S(2)}) collective-permute-start(f32[2,256,768]{2,1,0:T(8,128)} %get-tuple-element.24), channel_id=1, source_target_pairs={{0,4},{4,0},{8,12},{12,8},{16,20},{20,16},{24,28},{28,24},{1,5},{5... | collective-permute-start | bytes 4718600 | tf_op jit(solution)/shard_map/ppermute | solution.py:25
  13.6 8.8 %collective-permute-start.2 = (bf16[128,768]{1,0:T(8,128)(2,1)S(1)}, bf16[128,768]{1,0:T(8,128)(2,1)S(1)}, u32[]{:S(2)}, u32[]{:S(2)}) collective-permute-start(bf16[128,768]{1,0:T(8,128)(2,1)S(1)} %fusion.4), channel_id=1, source_target_pairs={{0,16},{4,20},{8,24},{12,28},{16,0},{20,4},{24,8},{28,12},{1,17},{... | collective-permute-start | bytes 589832 | tf_op jit(solution)/shard_map/ppermute | solution.py:25
  16.7 17.2 %collective-permute-start.1 = (f32[128,768]{1,0:T(8,128)S(1)}, f32[128,768]{1,0:T(8,128)S(1)}, u32[]{:S(2)}, u32[]{:S(2)}) collective-permute-start(f32[128,768]{1,0:T(8,128)S(1)} %slice_bitcast_fusion.1), channel_id=1, source_target_pairs={{0,16},{4,20},{8,24},{12,28},{16,0},{20,4},{24,8},{28,12},{1,17},{... | collective-permute-start | bytes 1179656 | tf_op jit(solution)/shard_map/ppermute | solution.py:25
  17.2 8.4 %collective-permute-start.10 = (bf16[128,768]{1,0:T(8,128)(2,1)S(1)}, bf16[128,768]{1,0:T(8,128)(2,1)S(1)}, u32[]{:S(2)}, u32[]{:S(2)}) collective-permute-start(bf16[128,768]{1,0:T(8,128)(2,1)S(1)} %fusion.5), channel_id=1, source_target_pairs={{0,8},{4,12},{8,0},{12,4},{16,24},{20,28},{24,16},{28,20},{1,9},{5... | collective-permute-start | bytes 589832 | tf_op jit(solution)/shard_map/ppermute | solution.py:25
  19.9 13.8 %collective-permute-start.9 = (f32[128,768]{1,0:T(8,128)S(1)}, f32[128,768]{1,0:T(8,128)S(1)}, u32[]{:S(2)}, u32[]{:S(2)}) collective-permute-start(f32[128,768]{1,0:T(8,128)S(1)} %slice_bitcast_fusion), channel_id=1, source_target_pairs={{0,8},{4,12},{8,0},{12,4},{16,24},{20,28},{24,16},{28,20},{1,9},{5... | collective-permute-start | bytes 1179656 | tf_op jit(solution)/shard_map/ppermute | solution.py:25
  34.0 4.7 %collective-permute-start.12 = (bf16[64,768]{1,0:T(8,128)(2,1)S(1)}, bf16[64,768]{1,0:T(8,128)(2,1)S(1)}, u32[]{:S(2)}, u32[]{:S(2)}) collective-permute-start(bf16[64,768]{1,0:T(8,128)(2,1)S(1)} %fusion.7), channel_id=1, source_target_pairs={{0,16},{4,20},{8,24},{12,28},{16,0},{20,4},{24,8},{28,12},{1,17},{... | collective-permute-start | bytes 294920 | tf_op jit(solution)/shard_map/ppermute | solution.py:25
  35.9 8.9 %collective-permute-start.4 = (bf16[64,768]{1,0:T(8,128)(2,1)S(1)}, bf16[64,768]{1,0:T(8,128)(2,1)S(1)}, u32[]{:S(2)}, u32[]{:S(2)}) collective-permute-start(bf16[64,768]{1,0:T(8,128)(2,1)S(1)} %fusion.6), channel_id=1, source_target_pairs={{0,8},{4,12},{8,0},{12,4},{16,24},{20,28},{24,16},{28,20},{1,9},{5... | collective-permute-start | bytes 294920 | tf_op jit(solution)/shard_map/ppermute | solution.py:25
  37.4 13.6 %collective-permute-start.3 = (f32[64,768]{1,0:T(8,128)S(1)}, f32[64,768]{1,0:T(8,128)S(1)}, u32[]{:S(2)}, u32[]{:S(2)}) collective-permute-start(f32[64,768]{1,0:T(8,128)S(1)} %slice_bitcast_fusion.3), channel_id=1, source_target_pairs={{0,8},{4,12},{8,0},{12,4},{16,24},{20,28},{24,16},{28,20},{1,9},{5... | collective-permute-start | bytes 589832 | tf_op jit(solution)/shard_map/ppermute | solution.py:25
  38.0 5.7 %collective-permute-start.11 = (f32[64,768]{1,0:T(8,128)S(1)}, f32[64,768]{1,0:T(8,128)S(1)}, u32[]{:S(2)}, u32[]{:S(2)}) collective-permute-start(f32[64,768]{1,0:T(8,128)S(1)} %slice_bitcast_fusion.2), channel_id=1, source_target_pairs={{0,16},{4,20},{8,24},{12,28},{16,0},{20,4},{24,8},{28,12},{1,17},{... | collective-permute-start | bytes 589832 | tf_op jit(solution)/shard_map/ppermute | solution.py:25
  43.7 5.7 %collective-permute-start.13 = (bf16[2,64,768]{2,1,0:T(8,128)(2,1)S(1)}, bf16[2,64,768]{2,1,0:T(8,128)(2,1)S(1)}, u32[]{:S(2)}, u32[]{:S(2)}) collective-permute-start(bf16[2,64,768]{2,1,0:T(8,128)(2,1)S(1)} %fusion.2), channel_id=1, source_target_pairs={{0,16},{4,20},{8,24},{12,28},{16,0},{20,4},{24,8},{28,12},{1,17},{... | collective-permute-start | bytes 589832 | tf_op jit(solution)/shard_map/ppermute | solution.py:25
  49.4 14.1 %collective-permute-start.14 = (bf16[2,128,768]{2,1,0:T(8,128)(2,1)S(1)}, bf16[2,128,768]{2,1,0:T(8,128)(2,1)S(1)}, u32[]{:S(2)}, u32[]{:S(2)}) collective-permute-start(bf16[2,128,768]{2,1,0:T(8,128)(2,1)S(1)} %pad_maximum_fusion.5), channel_id=1, source_target_pairs={{0,8},{4,12},{8,0},{12,4},{16,24},{20,28},{24,16},{28,20},{1,9},{5... | collective-permute-start | bytes 1179656 | tf_op jit(solution)/shard_map/ppermute | solution.py:25
  51.1 10.6 %collective-permute-start.5 = (bf16[2,64,768]{2,1,0:T(8,128)(2,1)S(1)}, bf16[2,64,768]{2,1,0:T(8,128)(2,1)S(1)}, u32[]{:S(2)}, u32[]{:S(2)}) collective-permute-start(bf16[2,64,768]{2,1,0:T(8,128)(2,1)S(1)} %fusion.3), channel_id=1, source_target_pairs={{0,8},{4,12},{8,0},{12,4},{16,24},{20,28},{24,16},{28,20},{1,9},{5... | collective-permute-start | bytes 589832 | tf_op jit(solution)/shard_map/ppermute | solution.py:25
  61.7 7.9 %collective-permute-start.6 = (bf16[2,128,768]{2,1,0:T(8,128)(2,1)S(1)}, bf16[2,128,768]{2,1,0:T(8,128)(2,1)S(1)}, u32[]{:S(2)}, u32[]{:S(2)}) collective-permute-start(bf16[2,128,768]{2,1,0:T(8,128)(2,1)S(1)} %pad_maximum_fusion.4), channel_id=1, source_target_pairs={{0,16},{4,20},{8,24},{12,28},{16,0},{20,4},{24,8},{28,12},{1,17},{... | collective-permute-start | bytes 1179656 | tf_op jit(solution)/shard_map/ppermute | solution.py:25
  63.6 6.1 %collective-permute-start.15 = (bf16[2,256,768]{2,1,0:T(8,128)(2,1)S(1)}, bf16[2,256,768]{2,1,0:T(8,128)(2,1)S(1)}, u32[]{:S(2)}, u32[]{:S(2)}) collective-permute-start(bf16[2,256,768]{2,1,0:T(8,128)(2,1)S(1)} %pad_maximum_fusion.1.low_ref), channel_id=1, source_target_pairs={{0,4},{4,0},{8,12},{12,8},{16,20},{20,16},{24,28},{28,24},{1,5},{5... | collective-permute-start | bytes 2359304 | tf_op jit(solution)/shard_map/ppermute | solution.py:25
  69.7 20.3 %copy-start.9 = (bf16[2,256,768]{2,1,0:T(8,128)(2,1)}, bf16[2,256,768]{2,1,0:T(8,128)(2,1)S(1)}, u32[]{:S(2)}) copy-start(bf16[2,256,768]{2,1,0:T(8,128)(2,1)S(1)} %pad_maximum_fusion.low_ref) | copy-start | bytes 2359300
  69.7 20.7 %collective-permute-start.7 = (bf16[2,256,768]{2,1,0:T(8,128)(2,1)S(1)}, bf16[2,256,768]{2,1,0:T(8,128)(2,1)S(1)}, u32[]{:S(2)}, u32[]{:S(2)}) collective-permute-start(bf16[2,256,768]{2,1,0:T(8,128)(2,1)S(1)} %pad_maximum_fusion.low_ref), channel_id=1, source_target_pairs={{0,4},{4,0},{8,12},{12,8},{16,20},{20,16},{24,28},{28,24},{1,5},{5... | collective-permute-start | bytes 2359304 | tf_op jit(solution)/shard_map/ppermute | solution.py:25
  90.0 20.8 %collective-permute-start.22 = (bf16[2,256,768]{2,1,0:T(8,128)(2,1)}, bf16[2,256,768]{2,1,0:T(8,128)(2,1)S(1)}, u32[]{:S(2)}, u32[]{:S(2)}) collective-permute-start(bf16[2,256,768]{2,1,0:T(8,128)(2,1)} %get-tuple-element.32), channel_id=1, source_target_pairs={{0,4},{4,0},{8,12},{12,8},{16,20},{20,16},{24,28},{28,24},{1,5},{5... | collective-permute-start | bytes 2359304 | tf_op jit(solution)/shard_map/ppermute | solution.py:25
  91.2 19.5 %copy-start.7 = (f32[2,256,768]{2,1,0:T(8,128)S(1)}, f32[2,256,768]{2,1,0:T(8,128)}, u32[]{:S(2)}) copy-start(f32[2,256,768]{2,1,0:T(8,128)} %get-tuple-element.31) | copy-start | bytes 4718596
  110.6 2.6 %collective-permute-start.16 = (bf16[2,256,768]{2,1,0:T(8,128)(2,1)}, bf16[2,256,768]{2,1,0:T(8,128)(2,1)S(1)}, u32[]{:S(2)}, u32[]{:S(2)}) collective-permute-start(bf16[2,256,768]{2,1,0:T(8,128)(2,1)} %get-tuple-element.30), channel_id=1, source_target_pairs={{0,4},{4,0},{8,12},{12,8},{16,20},{20,16},{24,28},{28,24},{1,5},{5... | collective-permute-start | bytes 2359304 | tf_op jit(solution)/shard_map/ppermute | solution.py:25
  111.0 11.4 %collective-permute-start.23 = (bf16[2,128,768]{2,1,0:T(8,128)(2,1)S(1)}, bf16[2,128,768]{2,1,0:T(8,128)(2,1)S(1)}, u32[]{:S(2)}, u32[]{:S(2)}) collective-permute-start(bf16[2,128,768]{2,1,0:T(8,128)(2,1)S(1)} %slice.175), channel_id=1, source_target_pairs={{0,8},{4,12},{8,0},{12,4},{16,24},{20,28},{24,16},{28,20},{1,9},{5... | collective-permute-start | bytes 1179656 | tf_op jit(solution)/shard_map/ppermute | solution.py:25
  113.3 11.2 %collective-permute-start.17 = (bf16[2,128,768]{2,1,0:T(8,128)(2,1)S(1)}, bf16[2,128,768]{2,1,0:T(8,128)(2,1)S(1)}, u32[]{:S(2)}, u32[]{:S(2)}) collective-permute-start(bf16[2,128,768]{2,1,0:T(8,128)(2,1)S(1)} %slice.176), channel_id=1, source_target_pairs={{0,16},{4,20},{8,24},{12,28},{16,0},{20,4},{24,8},{28,12},{1,17},{... | collective-permute-start | bytes 1179656 | tf_op jit(solution)/shard_map/ppermute | solution.py:25
  122.5 6.4 %collective-permute-start.24 = (bf16[2,64,768]{2,1,0:T(8,128)(2,1)S(1)}, bf16[2,64,768]{2,1,0:T(8,128)(2,1)S(1)}, u32[]{:S(2)}, u32[]{:S(2)}) collective-permute-start(bf16[2,64,768]{2,1,0:T(8,128)(2,1)S(1)} %slice.178), channel_id=1, source_target_pairs={{0,16},{4,20},{8,24},{12,28},{16,0},{20,4},{24,8},{28,12},{1,17},{... | collective-permute-start | bytes 589832 | tf_op jit(solution)/shard_map/ppermute | solution.py:25
  124.7 6.2 %collective-permute-start.18 = (bf16[2,64,768]{2,1,0:T(8,128)(2,1)S(1)}, bf16[2,64,768]{2,1,0:T(8,128)(2,1)S(1)}, u32[]{:S(2)}, u32[]{:S(2)}) collective-permute-start(bf16[2,64,768]{2,1,0:T(8,128)(2,1)S(1)} %slice.179), channel_id=1, source_target_pairs={{0,8},{4,12},{8,0},{12,4},{16,24},{20,28},{24,16},{28,20},{1,9},{5... | collective-permute-start | bytes 589832 | tf_op jit(solution)/shard_map/ppermute | solution.py:25
  128.9 5.7 %collective-permute-start.25 = (bf16[2,64,768]{2,1,0:T(8,128)(2,1)S(1)}, bf16[2,64,768]{2,1,0:T(8,128)(2,1)S(1)}, u32[]{:S(2)}, u32[]{:S(2)}) collective-permute-start(bf16[2,64,768]{2,1,0:T(8,128)(2,1)S(1)} %fusion), channel_id=1, source_target_pairs={{0,16},{4,20},{8,24},{12,28},{16,0},{20,4},{24,8},{28,12},{1,17},{... | collective-permute-start | bytes 589832 | tf_op jit(solution)/shard_map/ppermute | solution.py:25
  130.9 7.5 %collective-permute-start.19 = (bf16[2,64,768]{2,1,0:T(8,128)(2,1)S(1)}, bf16[2,64,768]{2,1,0:T(8,128)(2,1)S(1)}, u32[]{:S(2)}, u32[]{:S(2)}) collective-permute-start(bf16[2,64,768]{2,1,0:T(8,128)(2,1)S(1)} %fusion.1), channel_id=1, source_target_pairs={{0,8},{4,12},{8,0},{12,4},{16,24},{20,28},{24,16},{28,20},{1,9},{5... | collective-permute-start | bytes 589832 | tf_op jit(solution)/shard_map/ppermute | solution.py:25
  134.7 10.3 %collective-permute-start.26 = (bf16[2,128,768]{2,1,0:T(8,128)(2,1)S(1)}, bf16[2,128,768]{2,1,0:T(8,128)(2,1)S(1)}, u32[]{:S(2)}, u32[]{:S(2)}) collective-permute-start(bf16[2,128,768]{2,1,0:T(8,128)(2,1)S(1)} %pad_maximum_fusion.7), channel_id=1, source_target_pairs={{0,8},{4,12},{8,0},{12,4},{16,24},{20,28},{24,16},{28,20},{1,9},{5... | collective-permute-start | bytes 1179656 | tf_op jit(solution)/shard_map/ppermute | solution.py:25
  138.4 7.8 %collective-permute-start.20 = (bf16[2,128,768]{2,1,0:T(8,128)(2,1)S(1)}, bf16[2,128,768]{2,1,0:T(8,128)(2,1)S(1)}, u32[]{:S(2)}, u32[]{:S(2)}) collective-permute-start(bf16[2,128,768]{2,1,0:T(8,128)(2,1)S(1)} %pad_maximum_fusion.6), channel_id=1, source_target_pairs={{0,16},{4,20},{8,24},{12,28},{16,0},{20,4},{24,8},{28,12},{1,17},{... | collective-permute-start | bytes 1179656 | tf_op jit(solution)/shard_map/ppermute | solution.py:25
  145.1 3.7 %collective-permute-start.27 = (bf16[2,256,768]{2,1,0:T(8,128)(2,1)S(1)}, bf16[2,256,768]{2,1,0:T(8,128)(2,1)S(1)}, u32[]{:S(2)}, u32[]{:S(2)}) collective-permute-start(bf16[2,256,768]{2,1,0:T(8,128)(2,1)S(1)} %pad_maximum_fusion.3.low_ref), channel_id=1, source_target_pairs={{0,4},{4,0},{8,12},{12,8},{16,20},{20,16},{24,28},{28,24},{1,5},{5... | collective-permute-start | bytes 2359304 | tf_op jit(solution)/shard_map/ppermute | solution.py:25
  146.3 8.7 %collective-permute-start.21 = (bf16[2,256,768]{2,1,0:T(8,128)(2,1)S(1)}, bf16[2,256,768]{2,1,0:T(8,128)(2,1)S(1)}, u32[]{:S(2)}, u32[]{:S(2)}) collective-permute-start(bf16[2,256,768]{2,1,0:T(8,128)(2,1)S(1)} %pad_maximum_fusion.2.low_ref), channel_id=1, source_target_pairs={{0,4},{4,0},{8,12},{12,8},{16,20},{20,16},{24,28},{28,24},{1,5},{5... | collective-permute-start | bytes 2359304 | tf_op jit(solution)/shard_map/ppermute | solution.py:25
  163.0 11.6 %collective-permute-start.28 = (bf16[256,768]{1,0:T(8,128)(2,1)S(1)}, bf16[256,768]{1,0:T(8,128)(2,1)S(1)}, u32[]{:S(2)}, u32[]{:S(2)}) collective-permute-start(bf16[256,768]{1,0:T(8,128)(2,1)S(1)} %slice.174), channel_id=1, source_target_pairs={{0,1},{1,0},{2,3},{3,2},{4,5},{5,4},{6,7},{7,6},{8,9},{9,8},{10,11... | collective-permute-start | bytes 1179656 | tf_op jit(solution)/shard_map/ppermute | solution.py:25
  175.8 13.3 %collective-permute-start.29 = (bf16[128,768]{1,0:T(8,128)(2,1)S(1)}, bf16[128,768]{1,0:T(8,128)(2,1)S(1)}, u32[]{:S(2)}, u32[]{:S(2)}) collective-permute-start(bf16[128,768]{1,0:T(8,128)(2,1)S(1)} %slice.177), channel_id=1, source_target_pairs={{0,2},{1,3},{2,0},{3,1},{4,6},{5,7},{6,4},{7,5},{8,10},{9,11},{10,... | collective-permute-start | bytes 589832 | tf_op jit(solution)/shard_map/ppermute | solution.py:25
  (12 other events, 50.6 us)
